TPU v7x, 32 devices: a whole 2x2x4 slice. The times are simulated.
32 devices in a mesh: row: 4 (over y, x), col: 8 (over z, core).
Axes of the slice: x: 2, y: 2, z: 4, core: 2. Of those that a mesh axis runs over, the one named last changes fastest.
Arguments:
- source_blocks: float32 [8192, 24576], P('row', 'col'), may hold values from -6 to 6
Outputs:
- target_blocks: float32 [4096, 49152], P('row', 'col')
- column_sums: float32 [49152], P('col')
- frobenius: float32 [], replicated
All inputs are finite; a program needn't handle non-finite values.
Results may differ from a plain program's by a relative error of at most 0.00002.
Values sent between devices are 32-bit elements; how exact they have to be, the bound alone decides.
No kernel may reach another device: no remote copies, remote signals or barrier semaphores. Data moves between devices by JAX's collectives and lax.ppermute only.
A program may use at most 192 MiB of HBM per device.

v0:
```python
import math

import jax
import jax.numpy as jnp
from jax import lax
from jax.sharding import PartitionSpec as P

SB = 128


def swapped(value, axis, bit):
    mask = 2**bit
    pairs = [(source, source ^ mask) for source in range(lax.axis_size(axis))]
    return lax.ppermute(value, axis, pairs)


def halves(packed, dim_pos):
    first_half = lax.slice_in_dim(packed, 0, 1, axis=dim_pos)
    second_half = lax.slice_in_dim(packed, 1, 2, axis=dim_pos)
    return (first_half, second_half)


def rejoin(first_half, second_half, received, own_bit, dim_pos):
    low_part = jnp.where(own_bit == 0, first_half, received)
    high_part = jnp.where(own_bit == 0, received, second_half)
    return jnp.concatenate([low_part, high_part], axis=dim_pos)


def row_group_section(packed):
    row_count = lax.axis_size("row")
    groups = row_count // 4
    own_group = lax.axis_index("row") // 4
    moved = packed.transpose(1, 2, 0, 3, 4, 5, 6, 7)
    rest = moved.shape[2:]
    moved = moved.reshape((4,) + rest)
    marks = (jnp.arange(groups, dtype=jnp.int32) == own_group).reshape(
        (groups, 1) + (1,) * len(rest)
    )
    outgoing = jnp.where(marks, moved[None], jnp.zeros((), moved.dtype))
    outgoing = outgoing.reshape((row_count,) + rest)
    received = lax.all_to_all(outgoing, "row", split_axis=0, concat_axis=0, tiled=True)
    mine = lax.dynamic_slice_in_dim(received, own_group * 4, 4, 0)
    mine = mine.reshape((2, 2) + rest)
    return mine.transpose(2, 0, 1, 3, 4, 5, 6, 7)


def col_section(packed, bit_pos, dim_pos):
    own_bit = lax.axis_index("col") // (1 << bit_pos) % 2
    first_half, second_half = halves(packed, dim_pos)
    outgoing = jnp.where(own_bit == 0, second_half, first_half)
    received = swapped(outgoing, "col", bit_pos)
    return rejoin(first_half, second_half, received, own_bit, dim_pos)


def row_sections(packed):
    return row_group_section(packed)


def col_sections(packed):
    packed = col_section(packed, 0, 6)
    return col_section(packed, 1, 5)


def per_device(source_blocks):
    local_rows, local_cols = source_blocks.shape
    row_count = lax.axis_size("row")
    col_count = lax.axis_size("col")
    total_rows = local_rows * row_count
    total_cols = local_cols * col_count
    scale = 1.0 / math.sqrt(total_rows)
    blocks_down = local_rows // (8 * SB)
    blocks_across = local_cols // (2 * SB)
    packed = source_blocks.reshape(blocks_down, 2, 2, 2, SB, blocks_across, 2, SB)
    packed = packed.transpose(0, 2, 3, 4, 5, 1, 6, 7)
    packed = row_sections(packed)
    packed = col_sections(packed)
    target_blocks = packed.reshape(blocks_down * 4 * SB, blocks_across * 4 * SB)
    col_part = jnp.sum(target_blocks, axis=0)
    square_part = jnp.sum(target_blocks * target_blocks)
    row_cols, row_squares = lax.psum((col_part, square_part), "row")
    partner_cols = swapped(row_cols, "col", 1)
    squares_total = lax.psum(row_squares, "col")
    column_sums = (row_cols + partner_cols) * scale
    frobenius = jnp.sqrt(squares_total / (total_rows * total_cols))
    return (target_blocks, column_sums, frobenius)


def solution(mesh):
    return jax.shard_map(
        per_device,
        mesh=mesh,
        in_specs=(P("row", "col"),),
        out_specs=(P("row", "col"), P("col"), P()),
        check_vma=False,
    )
```

profile of v0, /device:TPU:0, one launch (start us, length us, event | category | flops | bytes accessed | tf_op | source)
XLA Modules:
  0.0 866.3 jit_solution(3515874479891333297)
XLA Ops:
  0.6 18.4 %broadcast_select_fusion.3 = f32[2048,3072]{1,0:T(8,128)} fusion(f32[2048,3072]{1,0:T(8,128)} %param.1, pred[]{:T(512)S(6)} %eq.20), kind=kLoop, calls=%fused_computation.9 | loop fusion | flops 6291456 | bytes 50331648 | tf_op jit(solution)/shard_map/jit(_where)/select_n | solution.py:39
  19.1 32.2 %select_n.75 = f32[2,2,2,2,128,12,2,128]{7,6,5,4,3,2,1,0:T(2,128)} reshape(f32[2048,3072]{1,0:T(8,128)} %broadcast_select_fusion.3) | data formatting | bytes 50331648 | tf_op jit(solution)/shard_map/jit(_where)/select_n | solution.py:39
  51.3 17.8 %copy.5 = f32[2,2,2,2,128,12,2,128]{7,6,1,5,4,0,3,2:T(2,128)} copy(f32[2,2,2,2,128,12,2,128]{7,6,5,4,3,2,1,0:T(2,128)} %select_n.75) | data formatting | bytes 50331648 | tf_op jit(solution)/shard_map/jit(_where)/select_n | solution.py:39
  69.1 8.4 all-to-all-start
  77.5 273.6 %all-to-all-done = f32[4,2,128,12,2,2,128]{6,5,4,3,2,1,0:T(2,128)} async-done(((f32[4,2,128,12,2,2,128]{6,5,4,3,2,1,0:T(2,128)}), f32[4,2,128,12,2,2,128]{6,5,4,3,2,1,0:T(2,128)}, u32[]{:S(2)}, u32[]{:S(2)}) %all-to-all-start) | async-done | bytes 25165856 | tf_op jit(solution)/shard_map/all_to_all | solution.py:41
  351.1 23.1 %broadcast_select_fusion.2 = f32[2,2,2,128,12,2,1,128]{7,6,5,4,3,0,2,1:T(1,128)} fusion(pred[]{:T(512)S(6)} %eq.19, f32[2,2,2,128,12,2,2,128]{7,6,5,4,3,0,2,1:T(2,128)} %bitcast.3), kind=kLoop, calls=%fused_computation.6 | loop fusion | flops 3145728 | bytes 37748736 | tf_op jit(solution)/shard_map/jit(_where)/select_n | solution.py:50
  374.2 0.1 collective-permute-start
  374.3 19.5 %collective-permute-done = f32[2,2,2,128,12,2,1,128]{7,6,5,4,3,0,2,1:T(1,128)} collective-permute-done((f32[2,2,2,128,12,2,1,128]{7,6,5,4,3,0,2,1:T(1,128)}, f32[2,2,2,128,12,2,1,128]{7,6,5,4,3,0,2,1:T(1,128)}, u32[]{:S(2)}, u32[]{:S(2)}) %collective-permute-start) | collective-permute-done | bytes 12582944 | tf_op jit(solution)/shard_map/ppermute | solution.py:14
  393.7 33.5 %broadcast_select_fusion.1 = (f32[2,2,2,128,12,2,1,128]{7,6,5,4,3,0,2,1:T(1,128)}, f32[2,2,2,128,12,2,1,128]{7,6,5,4,3,0,2,1:T(1,128)}) fusion(f32[2,2,2,128,12,2,1,128]{7,6,5,4,3,0,2,1:T(1,128)} %collective-permute-done, pred[]{:T(512)S(6)} %eq.19, f32[2,2,2,128,12,2,2,128]{7,6,5,4,3,0,2,1:T(2,128)} %bitcast.3), kind=kLoop, calls=%fused_computation.5 | loop fusion | flops 6291456 | bytes 62914560 | tf_op jit(solution)/shard_map/jit(_where)/select_n | solution.py:24
  427.3 22.3 %broadcast_select_fusion.6 = f32[2,2,2,128,12,1,2,128]{7,6,5,4,3,0,2,1:T(2,128)S(1)} fusion(pred[]{:T(512)S(6)} %eq.18, f32[2,2,2,128,12,2,1,128]{7,6,5,4,3,0,2,1:T(1,128)} %get-tuple-element.11, f32[2,2,2,128,12,2,1,128]{7,6,5,4,3,0,2,1:T(1,128)} %get-tuple-element.10), kind=kLoop, calls=%fused_computation.12 | loop fusion | flops 9437184 | bytes 37748736 | tf_op jit(solution)/shard_map/jit(_where)/select_n | solution.py:50
  449.6 1.9 collective-permute-start.1
  451.5 270.7 %collective-permute-done.1 = f32[2,2,2,128,12,1,2,128]{7,6,5,4,3,0,2,1:T(2,128)} collective-permute-done((f32[2,2,2,128,12,1,2,128]{7,6,5,4,3,0,2,1:T(2,128)S(1)}, f32[2,2,2,128,12,1,2,128]{7,6,5,4,3,0,2,1:T(2,128)}, u32[]{:S(2)}, u32[]{:S(2)}) %collective-permute-start.1) | collective-permute-done | bytes 12582944 | tf_op jit(solution)/shard_map/ppermute | solution.py:14
  722.2 32.0 %broadcast_select_fusion.5 = (f32[2,2,2,128,12,1,2,128]{7,6,5,4,3,0,2,1:T(2,128)}, f32[2,2,2,128,12,1,2,128]{7,6,5,4,3,0,2,1:T(2,128)}) fusion(f32[2,2,2,128,12,1,2,128]{7,6,5,4,3,0,2,1:T(2,128)} %collective-permute-done.1, pred[]{:T(512)S(6)} %eq.18, f32[2,2,2,128,12,2,1,128]{7,6,5,4,3,0,2,1:T(1,128)} %get-tuple-element.11, ...), kind=kLoop, calls=%fused_computation.11 | loop fusion | flops 12582912 | bytes 62914560 | tf_op jit(solution)/shard_map/jit(_where)/select_n | solution.py:24
  754.2 29.4 %multiply_reduce_fusion = (f32[]{:T(128)}, f32[12,2,2,128]{3,2,1,0:T(2,128)S(1)}, f32[2,2,2,128,12,2,2,128]{7,6,5,4,3,0,2,1:T(2,128)}) fusion(f32[2,2,2,128,12,1,2,128]{7,6,5,4,3,0,2,1:T(2,128)} %get-tuple-element.9, f32[2,2,2,128,12,1,2,128]{7,6,5,4,3,0,2,1:T(2,128)} %get-tuple-element.8), kind=kLoop, calls=%fused_computation.3 | loop fusion | flops 25159680 | bytes 50356228 | tf_op jit(solution)/shard_map/reduce_sum | solution.py:79
  783.6 16.3 %all-reduce = (f32[6144]{0:T(1024)S(1)}, f32[]{:T(128)}) all-reduce(f32[6144]{0:T(1024)S(1)} %bitcast.8, f32[]{:T(128)} %get-tuple-element.3), channel_id=1, replica_groups=mesh['row'=4,'col'=8] {'row'}, use_global_device_ids=true, to_apply=%region_1.2 | all-reduce | flops 6145 | bytes 49160 | tf_op jit(solution)/shard_map/psum | solution.py:80
  799.9 1.7 collective-permute-start.2
  801.6 14.2 %psum.23 = f32[]{:T(128)} all-reduce(f32[]{:T(128)} %get-tuple-element.6), channel_id=1, replica_groups=mesh['row'=4,'col'=8] {'col'}, use_global_device_ids=true, to_apply=%region_4.5 | all-reduce | flops 1 | bytes 8 | tf_op jit(solution)/shard_map/psum | solution.py:82
  816.5 17.5 %copy.6 = f32[2,2,2,128,12,2,2,128]{7,6,5,4,3,2,1,0:T(2,128)} copy(f32[2,2,2,128,12,2,2,128]{7,6,5,4,3,0,2,1:T(2,128)} %get-tuple-element.7) | data formatting | bytes 50331648 | tf_op jit(solution)/shard_map/concatenate | solution.py:26
  834.0 30.6 %reshape.33 = f32[1024,6144]{1,0:T(8,128)} reshape(f32[2,2,2,128,12,2,2,128]{7,6,5,4,3,2,1,0:T(2,128)} %copy.6) | data formatting | bytes 50331648 | tf_op jit(solution)/shard_map/reshape | solution.py:77
  864.6 0.0 collective-permute-done.2
  864.6 0.6 add_multiply_fusion
Async XLA Ops:
  69.1 282.0 %all-to-all-start = ((f32[4,2,128,12,2,2,128]{6,5,4,3,2,1,0:T(2,128)}), f32[4,2,128,12,2,2,128]{6,5,4,3,2,1,0:T(2,128)}, u32[]{:S(2)}, u32[]{:S(2)}) async-start(f32[4,2,128,12,2,2,128]{6,5,4,3,2,1,0:T(2,128)} %bitcast.7), calls=%async_computation | async-start | bytes 50331648 | tf_op jit(solution)/shard_map/all_to_all | solution.py:41
  374.2 19.6 %collective-permute-start = (f32[2,2,2,128,12,2,1,128]{7,6,5,4,3,0,2,1:T(1,128)}, f32[2,2,2,128,12,2,1,128]{7,6,5,4,3,0,2,1:T(1,128)}, u32[]{:S(2)}, u32[]{:S(2)}) collective-permute-start(f32[2,2,2,128,12,2,1,128]{7,6,5,4,3,0,2,1:T(1,128)} %broadcast_select_fusion.2), channel_id=1, source_target_pairs={{0,1},{1,0},{2,3},{3,2},{4,5},{5,4},{6,7},{7,6},{8,9},{9,8},{10,11... | collective-permute-start | bytes 37748744 | tf_op jit(solution)/shard_map/ppermute | solution.py:14
  449.6 272.6 %collective-permute-start.1 = (f32[2,2,2,128,12,1,2,128]{7,6,5,4,3,0,2,1:T(2,128)S(1)}, f32[2,2,2,128,12,1,2,128]{7,6,5,4,3,0,2,1:T(2,128)}, u32[]{:S(2)}, u32[]{:S(2)}) collective-permute-start(f32[2,2,2,128,12,1,2,128]{7,6,5,4,3,0,2,1:T(2,128)S(1)} %broadcast_select_fusion.6), channel_id=1, source_target_pairs={{0,2},{1,3},{2,0},{3,1},{4,6},{5,7},{6,4},{7,5},{8,10},{9,11},{10,... | collective-permute-start | bytes 37748744 | tf_op jit(solution)/shard_map/ppermute | solution.py:14
  799.9 64.7 %collective-permute-start.2 = (f32[6144]{0:T(1024)S(1)}, f32[6144]{0:T(1024)S(1)}, u32[]{:S(2)}, u32[]{:S(2)}) collective-permute-start(f32[6144]{0:T(1024)S(1)} %get-tuple-element.5), channel_id=1, source_target_pairs={{0,2},{1,3},{2,0},{3,1},{4,6},{5,7},{6,4},{7,5},{8,10},{9,11},{10,... | collective-permute-start | bytes 73736 | tf_op jit(solution)/shard_map/ppermute | solution.py:14
where the time goes:
time: 868 us; the launch traced here: 866 us
  waiting for transfers between devices  564 us (65%)
  other arithmetic  159 us (18%)
  local copies, waits for them, and re-layouts  98 us (11%)
  blocking collectives  30.6 us (4%)
  starting transfers between devices  12.1 us (1%)
    ppermute x3, waiting for transfers between devices, swapped(): return lax.ppermute(value, axis, pairs)  290 us
    all_to_all x1, waiting for transfers between devices, row_group_section(): lax.all_to_all(outgoing, 'row', split_axis=0, concat_axis=0, tiled=True)  274 us
    select_n x2, other arithmetic, rejoin(): low_part = jnp.where(own_bit == 0, first_half, received)  65.5 us
    select_n x2, local copies, waits for them, and re-layouts, row_group_section(): outgoing = jnp.where(marks, moved[None], jnp.zeros((), moved.dtype))  50 us
    select_n x2, other arithmetic, col_section(): outgoing = jnp.where(own_bit == 0, second_half, first_half)  45.4 us
    reshape x1, local copies, waits for them, and re-layouts, per_device(): target_blocks = packed.reshape(blocks_down * 4 * SB, blocks_across * 4 * SB)  30.6 us
    reduce_sum x1, other arithmetic, per_device(): square_part = jnp.sum(target_blocks * target_blocks)  29.4 us
    select_n x1, other arithmetic, row_group_section(): outgoing = jnp.where(marks, moved[None], jnp.zeros((), moved.dtype))  18.4 us
  transfers between devices with their start and end apart: 4, of which 3 were waited for; matrix products, arithmetic and copies ran while one was open for 6% of the time, Pallas kernels for 0%

commit v1 on v0

v1 whole, which is shorter than its diff:
```python
import math

import jax
import jax.numpy as jnp
from jax import lax
from jax.experimental import pallas as pl
from jax.experimental.pallas import tpu as pltpu
from jax.sharding import Mesh
from jax.sharding import PartitionSpec as P

SB = 128
ROWS = 16
PEERS = ("r4", "zlo", "core")


def pack_kernel(source, packed, sums, squares):
    @pl.when(pl.program_id(0) == 0)
    def _():
        sums[...] = jnp.zeros_like(sums)
        squares[...] = jnp.zeros_like(squares)

    blocks = source.shape[3] // (2 * SB)
    square = squares[...]
    for e in range(blocks):
        for core in range(2):
            lanes = pl.ds((2 * e + core) * SB, SB)
            total = sums[:, lanes]
            for s in range(8):
                value = source[0, s, :, lanes]
                packed[(s % 4) * 4 + (s // 4) * 2 + core, :, pl.ds(e * SB, SB)] = value
                grouped = value.reshape(ROWS // 8, 8, SB)
                total = total + jnp.sum(grouped, axis=0)
                square = square + jnp.sum(grouped * grouped, axis=0)
            sums[:, lanes] = total
    squares[...] = square


def pack(source, part):
    cols = source.shape[3]
    return pl.pallas_call(
        pack_kernel,
        grid=(SB // ROWS,),
        in_specs=[pl.BlockSpec((1, 8, ROWS, cols), lambda j: (part, 0, j, 0))],
        out_specs=[
            pl.BlockSpec((16, ROWS, cols // 2), lambda j: (0, j, 0)),
            pl.BlockSpec((8, cols), lambda j: (0, 0)),
            pl.BlockSpec((8, SB), lambda j: (0, 0)),
        ],
        out_shape=[
            jax.ShapeDtypeStruct((16, SB, cols // 2), jnp.float32),
            jax.ShapeDtypeStruct((8, cols), jnp.float32),
            jax.ShapeDtypeStruct((8, SB), jnp.float32),
        ],
        cost_estimate=pl.CostEstimate(
            flops=2 * 10**9, bytes_accessed=64 * SB * cols, transcendentals=0
        ),
        name=f"pack_{part}",
    )(source)


def place_kernel(*refs):
    received, target = refs[0], refs[-1]
    for e in range(received.shape[2] // SB):
        for p in range(4):
            for q in range(4):
                target[0, p, :, pl.ds((4 * e + q) * SB, SB)] = received[
                    p * 4 + q, :, pl.ds(e * SB, SB)
                ]


def place(received, target, part, parts):
    width = received.shape[2] * 4
    more = [] if target is None else [target]
    return pl.pallas_call(
        place_kernel,
        grid=(SB // ROWS,),
        in_specs=[pl.BlockSpec((16, ROWS, width // 4), lambda j: (0, j, 0))]
        + [pl.BlockSpec(memory_space=pl.ANY) for _ in more],
        out_specs=pl.BlockSpec((1, 4, ROWS, width), lambda j: (part, 0, j, 0)),
        out_shape=jax.ShapeDtypeStruct((parts, 4, SB, width), jnp.float32),
        input_output_aliases={1: 0} if more else {},
        cost_estimate=pl.CostEstimate(
            flops=2 * 10**9, bytes_accessed=32 * SB * width, transcendentals=0
        ),
        name=f"place_{part}",
    )(received, *more)


def per_device(source_blocks):
    local_rows, local_cols = source_blocks.shape
    row_count = lax.axis_size(("rg", "r4"))
    col_count = lax.axis_size(("chi", "zlo", "core"))
    total_rows = local_rows * row_count
    total_cols = local_cols * col_count
    scale = 1.0 / math.sqrt(total_rows)
    parts = local_rows // (8 * SB)
    source = source_blocks.reshape(parts, 8, SB, local_cols)
    received, sums, squares = [], 0.0, 0.0
    for part in range(parts):
        packed, part_sums, part_squares = pack(source, part)
        sums = sums + part_sums
        squares = squares + part_squares
        received.append(
            lax.all_to_all(packed, PEERS, split_axis=0, concat_axis=0, tiled=True)
        )
    target = None
    for part in range(parts):
        target = place(received[part], target, part, parts)
    target_blocks = target.reshape(parts * 4 * SB, 2 * local_cols)

    sums = jnp.sum(sums, axis=0)
    squares = jnp.broadcast_to(jnp.sum(squares), (SB,))
    partial = lax.psum(jnp.concatenate([sums, squares]), ("rg", "r4"))
    every = lax.all_gather(partial, ("chi", "zlo", "core"))
    frobenius = jnp.sqrt(jnp.sum(every[:, local_cols]) / (total_rows * total_cols))
    mine = lax.dynamic_slice_in_dim(every, lax.axis_index("chi") * 4, 4, 0)
    mine = mine[:, :local_cols].reshape(4, local_cols // (2 * SB), 2, SB)
    mine = lax.dynamic_index_in_dim(mine, lax.axis_index("core"), 2, False)
    column_sums = mine.transpose(1, 0, 2).reshape(2 * local_cols) * scale
    return (target_blocks, column_sums, frobenius)


def solution(mesh):
    rows, cols = mesh.shape["row"], mesh.shape["col"]
    grid = Mesh(
        mesh.devices.reshape(rows // 4, 4, cols // 4, 2, 2),
        ("rg", "r4", "chi", "zlo", "core"),
    )
    row, col = ("rg", "r4"), ("chi", "zlo", "core")
    return jax.shard_map(
        per_device,
        mesh=grid,
        in_specs=(P(row, col),),
        out_specs=(P(row, col), P(col), P()),
        check_vma=False,
    )
```

time: 868 us -> 375 us (0.43)
  waiting for transfers between devices: 564 us -> 138 us
  other arithmetic: 159 us -> 1.86 us
  blocking collectives: 30.6 us -> 171 us
  local copies, waits for them, and re-layouts: 98 us -> 0.72 us
  Pallas kernels: 0 us -> 48.5 us
    ppermute x3 -> x0, waiting for transfers between devices: 290 us -> none  [swapped(): return lax.ppermute(value, axis, pairs)]
    all_to_all x1 -> x2, waiting for transfers between devices: 274 us -> 138 us  [per_device(): lax.all_to_all(packed, PEERS, split_axis=0, concat_axis=0, tiled=True)]
    select_n x5 -> x0, other arithmetic: 129 us -> none  [the longest x2 65.5 us: rejoin(): low_part = jnp.where(own_bit == 0, first_half, received)]
    psum x2 -> x1, blocking collectives: 30.6 us -> 157 us  [per_device(): partial = lax.psum(jnp.concatenate([sums, squares]), ('rg', 'r4'))]
    select_n x2 -> x0, local copies, waits for them, and re-layouts: 50 us -> none  [row_group_section(): outgoing = jnp.where(marks, moved[None], jnp.zeros((), moved.dtype))]
    pallas_call x0 -> x4, Pallas kernels: none -> 48.5 us  [the longest x2 25.7 us: pack(): pl.pallas_call(pack_kernel, grid=(SB // ROWS,), in_specs=[pl.BlockSpec((1...]
    reshape x1 -> x0, local copies, waits for them, and re-layouts: 30.6 us -> none  [per_device(): target_blocks = packed.reshape(blocks_down * 4 * SB, blocks_across * 4 * SB)]
    reduce_sum x1 -> x3, other arithmetic: 29.4 us -> 1.24 us  [the longest x1 0.6 us: per_device(): jnp.sum(every[:, local_cols]) / (total_rows * total_cols)]
  transfers between devices with their start and end apart: 4 -> 2, of which waited for: 3 -> 1; matrix products, arithmetic and copies ran while one was open for 6% -> 1% of each run, Pallas kernels for 0% -> 6%
where the time goes in v1:
time: 375 us
  blocking collectives  171 us (46%)
  waiting for transfers between devices  138 us (37%)
  Pallas kernels  48.5 us (13%)
  starting transfers between devices  12.2 us (3%)
    psum x1, blocking collectives, per_device(): partial = lax.psum(jnp.concatenate([sums, squares]), ('rg', 'r4'))  157 us
    all_to_all x2, waiting for transfers between devices, per_device(): lax.all_to_all(packed, PEERS, split_axis=0, concat_axis=0, tiled=True)  138 us
    pallas_call x2, Pallas kernels, pack(): pl.pallas_call(pack_kernel, grid=(SB // ROWS,), in_specs=[pl.BlockSpec((1...  25.7 us
    pallas_call x2, Pallas kernels, place(): pl.pallas_call(place_kernel, grid=(SB // ROWS,), in_specs=[pl.BlockSpec((...  22.8 us
    all_gather x1, blocking collectives, per_device(): every = lax.all_gather(partial, ('chi', 'zlo', 'core'))  14.1 us
    all_to_all x2, starting transfers between devices, per_device(): lax.all_to_all(packed, PEERS, split_axis=0, concat_axis=0, tiled=True)  12.2 us
  transfers between devices with their start and end apart: 2, of which 1 were waited for; matrix products, arithmetic and copies ran while one was open for 1% of the time, Pallas kernels for 6%

profile of v1, /device:TPU:0, one launch (start us, length us, event | category | flops | bytes accessed | tf_op | source)
XLA Modules:
  0.0 374.5 jit_solution(7428627123227573998)
XLA Ops:
  0.6 12.8 %pack_0.1 = (f32[16,128,1536]{2,1,0:T(8,128)}, f32[8,3072]{1,0:T(8,128)}, f32[8,128]{1,0:T(8,128)}) custom-call(f32[2,8,128,3072]{3,2,1,0:T(8,128)} %bitcast.15), custom_call_target="tpu_custom_call" | custom-call | flops 2000000000 | bytes 25165824 | tf_op jit(solution)/shard_map/pack_0/pallas_call | solution.py:40
  13.5 6.4 %all-to-all-start.1 = ((f32[16,128,1536]{2,1,0:T(8,128)}), f32[16,128,1536]{2,1,0:T(8,128)}, u32[]{:S(2)}, u32[]{:S(2)}) async-start(f32[16,128,1536]{2,1,0:T(8,128)} %get-tuple-element.10), calls=%async_computation.1 | async-start | bytes 25165824 | tf_op jit(solution)/shard_map/all_to_all | solution.py:104
  19.8 12.8 %pack_1.1 = (f32[16,128,1536]{2,1,0:T(8,128)}, f32[8,3072]{1,0:T(8,128)}, f32[8,128]{1,0:T(8,128)}) custom-call(f32[2,8,128,3072]{3,2,1,0:T(8,128)} %bitcast.16), custom_call_target="tpu_custom_call" | custom-call | flops 2000000000 | bytes 25165824 | tf_op jit(solution)/shard_map/pack_1/pallas_call | solution.py:40
  32.7 137.8 %all-to-all-done.1.refs_0_ = f32[16,128,1536]{2,1,0:T(8,128)} async-done(((f32[16,128,1536]{2,1,0:T(8,128)}), f32[16,128,1536]{2,1,0:T(8,128)}, u32[]{:S(2)}, u32[]{:S(2)}) %all-to-all-start.1) | async-done | bytes 12582944 | tf_op jit(solution)/shard_map/all_to_all | solution.py:104
  170.5 0.0 copy-start.2
  170.5 0.0 copy-start.3
  170.5 0.0 copy-start
  170.5 0.0 copy-start.1
  170.5 5.9 %all-to-all-start = ((f32[16,128,1536]{2,1,0:T(8,128)}), f32[16,128,1536]{2,1,0:T(8,128)}, u32[]{:S(2)}, u32[]{:S(2)}) async-start(f32[16,128,1536]{2,1,0:T(8,128)} %get-tuple-element.9), calls=%async_computation | async-start | bytes 25165824 | tf_op jit(solution)/shard_map/all_to_all | solution.py:104
  176.4 0.0 copy-done.2
  176.4 0.0 copy-done.3
  176.4 0.6 add_reduce_fusion.1
  177.0 0.0 copy-done
  177.0 0.0 copy-done.1
  177.0 0.6 concatenate.3
  177.7 156.8 %psum.7 = f32[1,3200]{1,0:T(1,128)S(1)} all-reduce(f32[1,3200]{1,0:T(1,128)S(1)} %all_gather.6), channel_id=1, replica_groups=mesh['rg'=1,'r4'=4,'chi'=2,'zlo'=2,'core'=2] {'rg','r4'}, use_global_device_ids=true, to_apply=%region_2.0 | all-reduce | flops 3200 | bytes 25600 | tf_op jit(solution)/shard_map/psum | solution.py:113
  334.5 14.1 %all-gather = f32[8,1,3200]{2,1,0:T(1,128)S(1)} all-gather(f32[1,1,3200]{2,1,0:T(1,128)S(1)} %bitcast.21), channel_id=1, replica_groups=mesh['rg'=1,'r4'=4,'chi'=2,'zlo'=2,'core'=2] {'chi','zlo','core'}, dimensions={0}, use_global_device_ids=true | all-gather | bytes 115200 | tf_op jit(solution)/shard_map/all_gather | solution.py:114
  348.6 0.6 slice_reduce_fusion
  350.0 0.6 dynamic-slice_multiply_fusion
  350.6 11.4 %place_0.1.refs_1_ = f32[2,4,128,6144]{3,2,1,0:T(8,128)} custom-call(f32[16,128,1536]{2,1,0:T(8,128)} %all-to-all-done.1.refs_0_), custom_call_target="tpu_custom_call" | custom-call | flops 2000000000 | bytes 25165824 | tf_op jit(solution)/shard_map/place_0/pallas_call | solution.py:74
  362.0 0.0 all-to-all-done.refs_0_
  362.0 11.4 %place_1.1 = f32[2,4,128,6144]{3,2,1,0:T(8,128)} custom-call(f32[16,128,1536]{2,1,0:T(8,128)} %all-to-all-done.refs_0_, f32[2,4,128,6144]{3,2,1,0:T(8,128)} %place_0.1.refs_1_), custom_call_target="tpu_custom_call", output_to_operand_aliasing={{}: (1, {})} | custom-call | flops 2000000000 | bytes 25165824 | tf_op jit(solution)/shard_map/place_1/pallas_call | solution.py:74
  (6 shorter events, 0.1 us)
Async XLA Ops:
  13.5 157.0 %all-to-all-start.1 = ((f32[16,128,1536]{2,1,0:T(8,128)}), f32[16,128,1536]{2,1,0:T(8,128)}, u32[]{:S(2)}, u32[]{:S(2)}) async-start(f32[16,128,1536]{2,1,0:T(8,128)} %get-tuple-element.10), calls=%async_computation.1 | async-start | bytes 25165824 | tf_op jit(solution)/shard_map/all_to_all | solution.py:104
  170.5 5.9 %copy-start.2 = (f32[8,128]{1,0:T(8,128)S(1)}, f32[8,128]{1,0:T(8,128)}, u32[]{:S(2)}) copy-start(f32[8,128]{1,0:T(8,128)} %get-tuple-element.13) | copy-start | bytes 12292
  170.5 5.9 %copy-start.3 = (f32[8,128]{1,0:T(8,128)S(1)}, f32[8,128]{1,0:T(8,128)}, u32[]{:S(2)}) copy-start(f32[8,128]{1,0:T(8,128)} %get-tuple-element.14) | copy-start | bytes 12292
  170.5 6.5 %copy-start = (f32[8,3072]{1,0:T(8,128)S(1)}, f32[8,3072]{1,0:T(8,128)}, u32[]{:S(2)}) copy-start(f32[8,3072]{1,0:T(8,128)} %get-tuple-element.11) | copy-start | bytes 294916
  170.5 6.5 %copy-start.1 = (f32[8,3072]{1,0:T(8,128)S(1)}, f32[8,3072]{1,0:T(8,128)}, u32[]{:S(2)}) copy-start(f32[8,3072]{1,0:T(8,128)} %get-tuple-element.12) | copy-start | bytes 294916
  170.5 191.5 %all-to-all-start = ((f32[16,128,1536]{2,1,0:T(8,128)}), f32[16,128,1536]{2,1,0:T(8,128)}, u32[]{:S(2)}, u32[]{:S(2)}) async-start(f32[16,128,1536]{2,1,0:T(8,128)} %get-tuple-element.9), calls=%async_computation | async-start | bytes 25165824 | tf_op jit(solution)/shard_map/all_to_all | solution.py:104

commit v2 on v1

v2 whole, which is shorter than its diff:
```python
import math

import jax
import jax.numpy as jnp
from jax import lax
from jax.experimental import pallas as pl
from jax.sharding import Mesh
from jax.sharding import PartitionSpec as P

SB = 128
ROWS = 32
CHUNKS = 1
PEERS = ("r4", "zlo", "core")


def slab_rows(blocks):
    return (blocks // 8 + 1) * 8


def tree_sum(values):
    while len(values) > 1:
        values = [sum(values[i : i + 2]) for i in range(0, len(values), 2)]
    return values[0]


def pack_kernel(steps, tail, carried, *refs):
    source = refs[0]
    packed, sums, squares = refs[-3:]
    cols = source.shape[3]
    blocks = cols // (2 * SB)
    step = pl.program_id(0)

    @pl.when(step == 0)
    def _():
        if carried:
            sums[...] = refs[1][...]
            squares[...] = refs[2][...]
        else:
            sums[...] = jnp.zeros_like(sums)
            squares[...] = jnp.zeros_like(squares)

    @pl.when(step < steps)
    def _():
        square = [squares[...]] + [jnp.zeros((8, SB), jnp.float32)] * 3
        for e in range(blocks):
            for core in range(2):
                lanes = pl.ds((2 * e + core) * SB, SB)
                values = []
                for s in range(8):
                    peer = (s % 4) * 4 + (s // 4) * 2 + core
                    for o in range(ROWS // 8):
                        value = source[0, s, pl.ds(o * 8, 8), lanes]
                        packed[peer, pl.ds((o * blocks + e) * 8, 8), :] = value
                        values.append(value)
                for i in range(4):
                    square[i] = square[i] + tree_sum([v * v for v in values[i::4]])
                sums[:, lanes] = sums[:, lanes] + tree_sum(values)
        squares[...] = tree_sum(square)

    if tail:

        @pl.when(step == steps)
        def _():
            square = jnp.sum(squares[...], axis=0, keepdims=True)
            depth = slab_rows(blocks)
            for core in range(2):
                lines = [
                    jnp.sum(sums[:, pl.ds((2 * e + core) * SB, SB)], axis=0, keepdims=True)
                    for e in range(blocks)
                ]
                lines.append(square)
                lines.append(jnp.zeros((depth - blocks - 1, SB), jnp.float32))
                slab = jnp.concatenate([v for v in lines if v.shape[0]], axis=0)
                for peer in range(core, 16, 2):
                    packed[peer, pl.ds(0, depth), :] = slab


def pack(source, first, count, tail, carry):
    cols = source.shape[3]
    blocks = cols // (2 * SB)
    per = SB // ROWS
    steps = count * per
    depth = steps * ROWS * blocks + (slab_rows(blocks) if tail else 0)

    def at(j):
        j = jnp.minimum(j, steps - 1)
        return (first + j // per, 0, j % per, 0)

    whole = [
        pl.BlockSpec((8, cols), lambda j: (0, 0)),
        pl.BlockSpec((8, SB), lambda j: (0, 0)),
    ]
    return pl.pallas_call(
        lambda *refs: pack_kernel(steps, tail, bool(carry), *refs),
        grid=(steps + (1 if tail else 0),),
        in_specs=[pl.BlockSpec((1, 8, ROWS, cols), at)] + (whole if carry else []),
        out_specs=[
            pl.BlockSpec((16, ROWS * blocks, SB), lambda j: (0, j, 0)),
        ]
        + whole,
        out_shape=[
            jax.ShapeDtypeStruct((16, depth, SB), jnp.float32),
            jax.ShapeDtypeStruct((8, cols), jnp.float32),
            jax.ShapeDtypeStruct((8, SB), jnp.float32),
        ],
        cost_estimate=pl.CostEstimate(
            flops=2 * 10**9, bytes_accessed=64 * SB * cols, transcendentals=0
        ),
        name=f"pack_{first}",
    )(source, *carry)


def place_kernel(blocks, *refs):
    received, target = refs[0], refs[-1]
    for e in range(blocks):
        for p in range(4):
            for q in range(4):
                for o in range(ROWS // 8):
                    target[0, p, pl.ds(o * 8, 8), pl.ds((4 * e + q) * SB, SB)] = received[
                        p * 4 + q, pl.ds((o * blocks + e) * 8, 8), :
                    ]


def place(received, target, first, count, parts, blocks):
    width = blocks * 4 * SB
    per = SB // ROWS
    more = [] if target is None else [target]
    return pl.pallas_call(
        lambda *refs: place_kernel(blocks, *refs),
        grid=(count * per,),
        in_specs=[pl.BlockSpec((16, ROWS * blocks, SB), lambda j: (0, j, 0))]
        + [pl.BlockSpec(memory_space=pl.ANY) for _ in more],
        out_specs=pl.BlockSpec(
            (1, 4, ROWS, width), lambda j: (first + j // per, 0, j % per, 0)
        ),
        out_shape=jax.ShapeDtypeStruct((parts, 4, SB, width), jnp.float32),
        input_output_aliases={1: 0} if more else {},
        cost_estimate=pl.CostEstimate(
            flops=2 * 10**9, bytes_accessed=32 * SB * width, transcendentals=0
        ),
        name=f"place_{first}",
    )(received, *more)


def finish_kernel(blocks, scale, received, columns, squares):
    square = jnp.zeros((1, SB), jnp.float32)
    for q in range(4):
        total = tree_sum([received[p * 4 + q] for p in range(4)])
        for e in range(blocks):
            columns[pl.ds(4 * e + q, 1), :] = total[e : e + 1, :] * scale
        square = square + total[blocks : blocks + 1, :]
    squares[...] = square


def finish(received, blocks, scale):
    depth = slab_rows(blocks)
    last = received.shape[1] // depth - 1
    return pl.pallas_call(
        lambda *refs: finish_kernel(blocks, scale, *refs),
        grid=(1,),
        in_specs=[pl.BlockSpec((16, depth, SB), lambda j: (0, last, 0))],
        out_specs=[
            pl.BlockSpec((4 * blocks, SB), lambda j: (0, 0)),
            pl.BlockSpec((1, SB), lambda j: (0, 0)),
        ],
        out_shape=[
            jax.ShapeDtypeStruct((4 * blocks, SB), jnp.float32),
            jax.ShapeDtypeStruct((1, SB), jnp.float32),
        ],
        name="finish",
    )(received)


def per_device(source_blocks):
    local_rows, local_cols = source_blocks.shape
    row_count = lax.axis_size(("rg", "r4"))
    col_count = lax.axis_size(("chi", "zlo", "core"))
    total_rows = local_rows * row_count
    total_cols = local_cols * col_count
    blocks = local_cols // (2 * SB)
    parts = local_rows // (8 * SB)
    count = parts // CHUNKS
    source = source_blocks.reshape(parts, 8, SB, local_cols)
    received, carry = [], ()
    for first in range(0, parts, count):
        tail = first + count == parts
        packed, *carry = pack(source, first, count, tail, carry)
        received.append(
            lax.all_to_all(packed, PEERS, split_axis=0, concat_axis=0, tiled=True)
        )
    columns, squares = finish(received[-1], blocks, 1.0 / math.sqrt(total_rows))
    others = lax.axis_size(("rg", "chi"))
    total = squares
    for shift in range(1, others):
        pairs = [(i, (i + shift) % others) for i in range(others)]
        total = total + lax.ppermute(squares, ("rg", "chi"), pairs)
    if lax.axis_size("rg") > 1:
        columns = lax.psum(columns, "rg")
    target = None
    for i, first in enumerate(range(0, parts, count)):
        target = place(received[i], target, first, count, parts, blocks)
    target_blocks = target.reshape(parts * 4 * SB, 2 * local_cols)
    column_sums = columns.reshape(2 * local_cols)
    frobenius = jnp.sqrt(jnp.sum(total) / (total_rows * total_cols))
    return (target_blocks, column_sums, frobenius)


def solution(mesh):
    rows, cols = mesh.shape["row"], mesh.shape["col"]
    grid = Mesh(
        mesh.devices.reshape(rows // 4, 4, cols // 4, 2, 2),
        ("rg", "r4", "chi", "zlo", "core"),
    )
    row, col = ("rg", "r4"), ("chi", "zlo", "core")
    return jax.shard_map(
        per_device,
        mesh=grid,
        in_specs=(P(row, col),),
        out_specs=(P(row, col), P(col), P()),
        check_vma=False,
    )
```

time: 375 us -> 331 us (0.88)
  waiting for transfers between devices: 138 us -> 0.01 us
  blocking collectives: 171 us -> 284 us
  starting transfers between devices: 12.2 us -> 3.32 us
  Pallas kernels: 48.5 us -> 40 us
    all_to_all x0 -> x1, blocking collectives: none -> 284 us  [per_device(): lax.all_to_all(packed, PEERS, split_axis=0, concat_axis=0, tiled=True)]
    psum x1 -> x0, blocking collectives: 157 us -> none  [per_device(): partial = lax.psum(jnp.concatenate([sums, squares]), ('rg', 'r4'))]
    all_to_all x2 -> x0, waiting for transfers between devices: 138 us -> none  [per_device(): lax.all_to_all(packed, PEERS, split_axis=0, concat_axis=0, tiled=True)]
    all_gather x1 -> x0, blocking collectives: 14.1 us -> none  [per_device(): every = lax.all_gather(partial, ('chi', 'zlo', 'core'))]
    all_to_all x2 -> x0, starting transfers between devices: 12.2 us -> none  [per_device(): lax.all_to_all(packed, PEERS, split_axis=0, concat_axis=0, tiled=True)]
    pallas_call x4 -> x3, Pallas kernels: 48.5 us -> 40 us  [the longest x1 20 us: pack(): pl.pallas_call(lambda *refs: pack_kernel(steps, tail, bool(carry), *refs)...]
  transfers between devices with their start and end apart: 2 -> 1, of which waited for: 1 -> 0; matrix products, arithmetic and copies ran while one was open for 1% -> 0% of each run, Pallas kernels for 6% -> 6%
where the time goes in v2:
time: 331 us; the launch traced here: 330 us
  blocking collectives  284 us (86%)
  Pallas kernels  40 us (12%)
  starting transfers between devices  3.32 us (1%)
    all_to_all x1, blocking collectives, per_device(): lax.all_to_all(packed, PEERS, split_axis=0, concat_axis=0, tiled=True)  284 us
    pallas_call x1, Pallas kernels, pack(): pl.pallas_call(lambda *refs: pack_kernel(steps, tail, bool(carry), *refs)...  20 us
    pallas_call x1, Pallas kernels, place(): pl.pallas_call(lambda *refs: place_kernel(blocks, *refs), grid=(count * p...  18.4 us
  transfers between devices with their start and end apart: 1, of which 0 were waited for; matrix products, arithmetic and copies ran while one was open for 0% of the time, Pallas kernels for 6%

profile of v2, /device:TPU:0, one launch (start us, length us, event | category | flops | bytes accessed | tf_op | source)
XLA Modules:
  0.0 330.0 jit_solution(11266383648128986868)
XLA Ops:
  0.6 20.0 %pack_0.1 = (f32[16,3088,128]{2,1,0:T(8,128)}, f32[8,3072]{1,0:T(8,128)}, f32[8,128]{1,0:T(8,128)}) custom-call(f32[2,8,128,3072]{3,2,1,0:T(8,128)} %bitcast.3), custom_call_target="tpu_custom_call" | custom-call | flops 2000000000 | bytes 25165824 | tf_op jit(solution)/shard_map/pack_0/pallas_call | solution.py:93
  20.7 283.7 %all_to_all.5.refs_0_ = f32[16,3088,128]{2,1,0:T(8,128)} all-to-all(f32[16,3088,128]{2,1,0:T(8,128)} %get-tuple-element.6), channel_id=1, replica_groups=mesh['rg'=1,'r4'=4,'chi'=2,'zlo'=2,'core'=2] {'r4','zlo','core'}, dimensions={0} | all-to-all | bytes 50593792 | tf_op jit(solution)/shard_map/all_to_all | solution.py:189
  304.3 1.5 finish.1
  305.9 0.0 copy-start
  305.9 3.3 %collective-permute-start = (f32[1,128]{1,0:T(1,128)}, f32[1,128]{1,0:T(1,128)S(1)}, u32[]{:S(2)}, u32[]{:S(2)}) collective-permute-start(f32[1,128]{1,0:T(1,128)} %get-tuple-element.8), channel_id=1, source_target_pairs={{0,4},{4,0},{1,5},{5,1},{2,6},{6,2},{3,7},{7,3},{8,12},{12,8},{9,1... | collective-permute-start | bytes 1544 | tf_op jit(solution)/shard_map/ppermute | solution.py:196
  309.2 18.4 %place_0.1 = f32[2,4,128,6144]{3,2,1,0:T(8,128)} custom-call(f32[16,3088,128]{2,1,0:T(8,128)} %all_to_all.5.refs_0_), custom_call_target="tpu_custom_call" | custom-call | flops 2000000000 | bytes 25165824 | tf_op jit(solution)/shard_map/place_0/pallas_call | solution.py:128
  327.6 0.0 collective-permute-done
  327.6 0.0 copy-done
  327.6 0.6 add_reduce_fusion
Async XLA Ops:
  305.9 21.7 %copy-start = (f32[1,128]{1,0:T(1,128)S(1)}, f32[1,128]{1,0:T(1,128)}, u32[]{:S(2)}) copy-start(f32[1,128]{1,0:T(1,128)} %get-tuple-element.8) | copy-start | bytes 1540
  305.9 21.7 %collective-permute-start = (f32[1,128]{1,0:T(1,128)}, f32[1,128]{1,0:T(1,128)S(1)}, u32[]{:S(2)}, u32[]{:S(2)}) collective-permute-start(f32[1,128]{1,0:T(1,128)} %get-tuple-element.8), channel_id=1, source_target_pairs={{0,4},{4,0},{1,5},{5,1},{2,6},{6,2},{3,7},{7,3},{8,12},{12,8},{9,1... | collective-permute-start | bytes 1544 | tf_op jit(solution)/shard_map/ppermute | solution.py:196
